TPU v7x, 32 devices: a whole 2x2x4 slice. The times are simulated.
32 devices in a mesh: grp: 4 (over y, core), ep: 8 (over z, x).
Axes of the slice: x: 2, y: 2, z: 4, core: 2. Of those that a mesh axis runs over, the one named last changes fastest.
Arguments:
- d_out: bfloat16 [4096, 2048], P(('grp', 'ep')), may hold values from -12 to 12
- routes: int32 [4096, 2], P(('grp', 'ep')), may hold values from 0 to 7, all different within a row; in each aligned block of 128 rows (0 to 127, 128 to 255, ...) at most 48 rows name the same one
- combine: float32 [4096, 2], P(('grp', 'ep')), may hold values from 0.05 to 1
- live_tokens: int32 [32], P(('grp', 'ep')), may hold values from 1 to 128, as said below
- hidden: bfloat16 [1536, 57344], P('grp', 'ep'), may hold values from -6 to 6
Outputs:
- expert_grad: float32 [2048, 57344], P('grp', 'ep')
Inputs may be any that keep to these rules, and one draw needn't show every extreme that they name: `routes`: the two experts of a token differ. Among the 128 rows of one device no expert is named by more than 48 rows, and on some devices one expert is named by exactly 48 rows. `live_tokens`: the live tokens of a device are its first ones; on the last device all 128 are live.
All inputs are finite; a program needn't handle non-finite values.
Results may differ from a plain program's by a relative error of at most 0.0029.
Values may be sent and summed in bfloat16 or wider, within the bound.
A program may use at most 128 MiB of HBM per device.

v0:
```python
import functools

import jax
import jax.numpy as jnp
from jax import lax
from jax.experimental import pallas as pl
from jax.experimental.pallas import tpu as pltpu
from jax.sharding import PartitionSpec as P

EXPERTS = 8
CAP = 48
CORES = 2
CHUNKS = 7
MESH = pl.DeviceIdType.MESH


def pick_chunks(columns):
    return CHUNKS if columns % (CHUNKS * 128) == 0 else 1


def counts_kernel(n_grp, n_ep, ladder, router, live, sel, info, table, grp_send, grp_recv, ep_send, ep_recv):
    grp, ep = lax.axis_index("grp"), lax.axis_index("ep")
    shards = n_ep // EXPERTS
    barrier = pltpu.get_barrier_semaphore()

    def in_grp(j):
        return {"grp": lax.rem(grp + j, n_grp), "ep": ep}

    def in_ep(j):
        return {"grp": grp, "ep": lax.rem(ep + j, n_ep)}

    for j in range(1, n_grp):
        pl.semaphore_signal(barrier, inc=1, device_id=in_grp(j), device_id_type=MESH)
    for j in range(1, n_ep):
        pl.semaphore_signal(barrier, inc=1, device_id=in_ep(j), device_id_type=MESH)
    tokens, top = router.shape[0], router.shape[1] // 2
    lanes = lax.broadcasted_iota(jnp.int32, (tokens, 128), 1).astype(jnp.float32)
    alive = lax.broadcasted_iota(jnp.int32, (tokens, 128), 0) < live[0]
    hits = jnp.zeros((tokens, 128), jnp.float32)
    for k in range(top):
        hits = hits + jnp.where((router[:, k : k + 1] == lanes) & alive, 1.0, 0.0)
    table[ep, grp] = jnp.broadcast_to(jnp.sum(hits, axis=0, keepdims=True), (8, 128))
    pl.semaphore_wait(barrier, n_grp - 1 + n_ep - 1)

    def grp_copy(j, owner):
        part = table.at[ep, owner]
        return pltpu.make_async_remote_copy(
            src_ref=part, dst_ref=part, send_sem=grp_send.at[j], recv_sem=grp_recv.at[j],
            device_id=in_grp(j), device_id_type=MESH)

    def ep_copy(j, owner):
        part = table.at[owner]
        return pltpu.make_async_remote_copy(
            src_ref=part, dst_ref=part, send_sem=ep_send.at[j], recv_sem=ep_recv.at[j],
            device_id=in_ep(j), device_id_type=MESH)

    for j in range(1, n_grp):
        grp_copy(j, grp).start()
    for j in range(1, n_grp):
        grp_copy(j, lax.rem(grp - j + n_grp, n_grp)).wait_recv()
    for j in range(1, n_ep):
        ep_copy(j, ep).start()
    for j in range(1, n_ep):
        ep_copy(j, lax.rem(ep - j + n_ep, n_ep)).wait_recv()

    mine = lax.broadcasted_iota(jnp.int32, (1, 128), 1) == ep // shards
    slots = sel.shape[1]
    slot = lax.broadcasted_iota(jnp.int32, (1, slots), 1)
    source = slot // CAP
    place = (slot - source * CAP).astype(jnp.float32)
    filled = jnp.zeros((1, slots), jnp.float32)
    first = jnp.zeros((1, slots), jnp.float32)
    for s in range(n_ep):
        amount = jnp.sum(jnp.where(mine, table[s, grp, 0:1, :], 0.0), axis=1, keepdims=True)
        filled = filled + jnp.where(source == s, amount, 0.0)
        first = first + jnp.where(source > s, amount, 0.0)
    target = jnp.where(place < filled, first + place, -1.0)
    rows = 64 if slots % 64 == 0 else slots

    def write(i, _):
        start = pl.multiple_of(i * rows, rows)
        index = (lax.broadcasted_iota(jnp.int32, (rows, slots), 0) + start).astype(jnp.float32)
        sel[pl.ds(start, rows), :] = jnp.where(index == target, 1.0, 0.0).astype(sel.dtype)
        return 0

    lax.fori_loop(0, slots // rows, write, 0)
    need = [jnp.zeros((1, 128), jnp.float32) for _ in range(CORES)]
    count = jnp.zeros((1, 128), jnp.float32)
    for g in range(n_grp):
        used = jnp.zeros((1, 128), jnp.float32)
        for s in range(n_ep):
            used = used + table[s, g, 0:1, :]
        need[g % CORES] = jnp.maximum(need[g % CORES], used)
        count = count + used
    count = jnp.sum(jnp.where(mine, count, 0.0), axis=1, keepdims=True)
    need = [jnp.max(n, axis=1, keepdims=True) for n in need]
    branch = jnp.zeros((1, 1), jnp.float32)
    for keep in ladder:
        branch = branch + jnp.where((need[0] <= keep[0]) & (need[1] <= keep[1]), 0.0, 1.0)
    lane = lax.broadcasted_iota(jnp.int32, (8, 128), 1)
    info[...] = jnp.where(lane == 0, branch, count)
    for j in range(1, n_grp):
        grp_copy(j, grp).wait_send()
    for j in range(1, n_ep):
        ep_copy(j, ep).wait_send()


def share_counts(router, live, slots, ladder, n_grp, n_ep):
    dma = pltpu.SemaphoreType.DMA
    return pl.pallas_call(
        functools.partial(counts_kernel, n_grp, n_ep, ladder),
        out_shape=(
            jax.ShapeDtypeStruct((slots, slots), jnp.bfloat16),
            jax.ShapeDtypeStruct((8, 128), jnp.float32),
        ),
        in_specs=[pl.BlockSpec(memory_space=pltpu.VMEM), pl.BlockSpec(memory_space=pltpu.SMEM)],
        out_specs=(pl.BlockSpec(memory_space=pltpu.VMEM), pl.BlockSpec(memory_space=pltpu.VMEM)),
        scratch_shapes=[
            pltpu.VMEM((n_ep, n_grp, 8, 128), jnp.float32),
            dma((n_grp,)), dma((n_grp,)), dma((n_ep,)), dma((n_ep,)),
        ],
        compiler_params=pltpu.CompilerParams(collective_id=0, has_side_effects=True),
        name="share_counts",
    )(router, live)


def exchange_kernel(n_grp, n_ep, keep, sel, d_out, router, live, hidden, all_hidden, all_rows, buffer, arrived, packed, packed_rows,
                    slot_send, slot_recv, slot_own, far_send, far_recv, near_send, near_recv,
                    relay_send, relay_recv, row_send, row_recv, own_sem):
    n_y = n_grp // CORES
    grp, ep = lax.axis_index("grp"), lax.axis_index("ep")
    shards = n_ep // EXPERTS
    y = grp // CORES
    core = lax.rem(grp, CORES)
    pair = keep[0] + keep[1]
    chunks = pick_chunks(hidden.shape[1])
    wide = hidden.shape[1] // chunks
    block = all_rows.shape[1]

    barrier = pltpu.get_barrier_semaphore()

    def greet_ep(j, _):
        pl.semaphore_signal(barrier, inc=1, device_id={"grp": grp, "ep": lax.rem(ep + j, n_ep)}, device_id_type=MESH)
        return 0

    def greet_grp(j, _):
        pl.semaphore_signal(barrier, inc=1, device_id={"grp": lax.rem(grp + j, n_grp), "ep": ep}, device_id_type=MESH)
        return 0

    lax.fori_loop(1, n_ep, greet_ep, 0)
    lax.fori_loop(1, n_grp, greet_grp, 0)
    pl.semaphore_wait(barrier, n_ep - 1 + n_grp - 1)

    def expert_slots(expert):
        return buffer.at[pl.ds(pl.multiple_of(expert * CAP, CAP), CAP), :]

    def slot_copy(j, source):
        target = lax.rem(ep + j, n_ep)
        return pltpu.make_async_remote_copy(
            src_ref=expert_slots(target // shards),
            dst_ref=arrived.at[pl.ds(pl.multiple_of(source * CAP, CAP), CAP), :],
            send_sem=slot_send.at[j], recv_sem=slot_recv.at[j],
            device_id={"grp": grp, "ep": target}, device_id_type=MESH)

    def slot_start(j, _):
        slot_copy(j, ep).start()
        return 0

    def slot_finish(j, _):
        slot_copy(j, ep).wait_send()
        slot_copy(j, lax.rem(ep - j + n_ep, n_ep)).wait_recv()
        return 0

    slot_mine = pltpu.make_async_copy(
        expert_slots(ep // shards), arrived.at[pl.ds(pl.multiple_of(ep * CAP, CAP), CAP), :], slot_own)

    def fill_slots():
        tokens, top = router.shape[0], router.shape[1] // 2
        lanes = lax.broadcasted_iota(jnp.int32, (tokens, 128), 1).astype(jnp.float32)
        alive = jnp.where(lax.broadcasted_iota(jnp.int32, (tokens, 1), 0) < live[0], 1.0, 0.0)
        chosen = [jnp.where(router[:, k : k + 1] == lanes, 1.0, 0.0) for k in range(top)]
        square = (tokens, tokens)
        earlier = jnp.where(
            lax.broadcasted_iota(jnp.int32, square, 0) > lax.broadcasted_iota(jnp.int32, square, 1), 1.0, 0.0)
        running = jnp.dot(
            earlier.astype(jnp.bfloat16), sum(chosen).astype(jnp.bfloat16), preferred_element_type=jnp.float32)
        slot = lax.broadcasted_iota(jnp.int32, (tokens, EXPERTS * CAP), 1).astype(jnp.float32)
        puts, weights = [], []
        for k in range(top):
            position = jnp.sum(chosen[k] * running, axis=1, keepdims=True)
            running = running + chosen[k]
            place = router[:, k : k + 1] * CAP + position
            puts.append(jnp.where(slot == place, 1.0, 0.0).astype(jnp.bfloat16))
            weights.append(router[:, top + k : top + k + 1] * alive)
        for i in range(n_grp):
            part = slice(i * block, (i + 1) * block)
            rows = d_out[:, part].astype(jnp.float32)
            buffer[:, part] = sum(
                lax.dot_general(
                    put, (rows * weight).astype(jnp.bfloat16), (((0,), (0,)), ((), ())),
                    preferred_element_type=jnp.float32)
                for put, weight in zip(puts, weights)).astype(d_out.dtype)

    def path(which):
        mine, other = keep[which], keep[1 - which]
        mate = y * CORES + (1 - which)

        def span(row, cell):
            start = row * pair + (0 if cell == 0 else keep[0])
            return pl.ds(pl.multiple_of(start, 16), keep[cell])

        def columns(i):
            return pl.ds(pl.multiple_of(i * wide, 128), wide)

        def at_y(j):
            return {"grp": lax.rem(y + j, n_y) * CORES + which, "ep": ep}

        def own_copy(i):
            return pltpu.make_async_copy(
                packed.at[pl.ds(0, mine), columns(i)], all_hidden.at[span(y, which), columns(i)], own_sem.at[i])

        def far_copy(j, i, row):
            return pltpu.make_async_remote_copy(
                src_ref=packed.at[pl.ds(0, mine), columns(i)], dst_ref=all_hidden.at[span(row, which), columns(i)],
                send_sem=far_send.at[j, i], recv_sem=far_recv.at[j, i], device_id=at_y(j), device_id_type=MESH)

        def near_copy(i):
            return pltpu.make_async_remote_copy(
                src_ref=packed.at[pl.ds(0, mine), columns(i)], dst_ref=all_hidden.at[span(y, which), columns(i)],
                send_sem=near_send.at[i], recv_sem=near_recv.at[i],
                device_id={"grp": mate, "ep": ep}, device_id_type=MESH)

        def near_arrival(i):
            return pltpu.make_async_remote_copy(
                src_ref=all_hidden.at[span(y, 1 - which), columns(i)],
                dst_ref=all_hidden.at[span(y, 1 - which), columns(i)],
                send_sem=near_send.at[i], recv_sem=near_recv.at[i],
                device_id={"grp": mate, "ep": ep}, device_id_type=MESH)

        def relay_copy(j, i, cell):
            row = lax.rem(y - j + n_y, n_y)
            return pltpu.make_async_remote_copy(
                src_ref=all_hidden.at[span(row, cell), columns(i)], dst_ref=all_hidden.at[span(row, cell), columns(i)],
                send_sem=relay_send.at[j, i], recv_sem=relay_recv.at[j, i],
                device_id={"grp": mate, "ep": ep}, device_id_type=MESH)

        def row_copy(j, k):
            cell = which if k == 0 else 1 - which
            target = lax.rem(y + j, n_y) * CORES + cell
            return pltpu.make_async_remote_copy(
                src_ref=packed_rows.at[pl.ds(0, mine), pl.ds(pl.multiple_of(target * block, 128), block)],
                dst_ref=all_rows.at[span(y, which), :],
                send_sem=row_send.at[j, k], recv_sem=row_recv.at[j, k],
                device_id={"grp": target, "ep": ep}, device_id_type=MESH)

        def row_arrival(j, k):
            cell = which if k == 0 else 1 - which
            here = all_rows.at[span(lax.rem(y - j + n_y, n_y), cell), :]
            return pltpu.make_async_remote_copy(
                src_ref=here, dst_ref=here, send_sem=row_send.at[j, k], recv_sem=row_recv.at[j, k],
                device_id={"grp": lax.rem(grp + 1, n_grp), "ep": ep}, device_id_type=MESH)

        others = [(j, k) for j in range(n_y) for k in range(CORES) if (j, k) != (0, 0)]

        def start(i):
            for j in range(1, n_y):
                far_copy(j, i, y).start()
            near_copy(i).start()
            own_copy(i).start()

        def pack(i, _):
            packed[pl.ds(0, mine), columns(i)] = jnp.dot(
                sel[pl.ds(0, mine), :], hidden[:, columns(i)], preferred_element_type=jnp.float32).astype(packed.dtype)

            @pl.when(i > 0)
            def _():
                start(i - 1)

            return 0

        def relay(i, _):
            for j in range(1, n_y):
                far_copy(j, i, lax.rem(y - j + n_y, n_y)).wait_recv()
                relay_copy(j, i, which).start()
            return 0

        stops = [min(i, chunks) for i in range(4)] + [chunks]
        lax.fori_loop(0, chunks, pack, 0)
        fill_slots()
        start(chunks - 1)
        lax.fori_loop(stops[0], stops[1], relay, 0)
        lax.fori_loop(1, n_ep, slot_start, 0)
        slot_mine.start()
        lax.fori_loop(stops[1], stops[2], relay, 0)
        lax.fori_loop(1, n_ep, slot_finish, 0)
        slot_mine.wait()

        def pack_rows(i, _):
            part = pl.ds(pl.multiple_of(i * block, 128), block)
            packed_rows[pl.ds(0, mine), part] = jnp.dot(
                sel[pl.ds(0, mine), :], arrived[:, part], preferred_element_type=jnp.float32).astype(packed_rows.dtype)
            return 0

        lax.fori_loop(0, n_grp, pack_rows, 0)
        lax.fori_loop(stops[2], stops[3], relay, 0)
        row_mine = pltpu.make_async_copy(
            packed_rows.at[pl.ds(0, mine), pl.ds(pl.multiple_of(grp * block, 128), block)],
            all_rows.at[span(y, which), :], own_sem.at[chunks])
        for j, k in others:
            row_copy(j, k).start()
        row_mine.start()

        lax.fori_loop(stops[3], stops[4], relay, 0)

        def finish(i, _):
            own_copy(i).wait()
            near_copy(i).wait_send()
            near_arrival(i).wait_recv()
            for j in range(1, n_y):
                far_copy(j, i, y).wait_send()
                relay_copy(j, i, which).wait_send()
                relay_copy(j, i, 1 - which).wait_recv()
            return 0

        lax.fori_loop(0, chunks, finish, 0)
        for j, k in others:
            row_copy(j, k).wait_send()
            row_arrival(j, k).wait_recv()
        row_mine.wait()

    for which in range(CORES):
        pl.when(core == which)(functools.partial(path, which))


def exchange(number, keep, sel, d_out, router, live, hidden, n_grp, n_ep):
    n_y = n_grp // CORES
    most = max(keep)
    slots, columns = hidden.shape
    width = d_out.shape[1]
    chunks = pick_chunks(columns)
    rows = n_y * (keep[0] + keep[1])
    dma = pltpu.SemaphoreType.DMA
    return pl.pallas_call(
        functools.partial(exchange_kernel, n_grp, n_ep, keep),
        out_shape=(
            jax.ShapeDtypeStruct((rows, columns), hidden.dtype),
            jax.ShapeDtypeStruct((rows, width // n_grp), d_out.dtype),
        ),
        in_specs=[
            pl.BlockSpec(memory_space=pltpu.VMEM),
            pl.BlockSpec(memory_space=pltpu.VMEM),
            pl.BlockSpec(memory_space=pltpu.VMEM),
            pl.BlockSpec(memory_space=pltpu.SMEM),
            pl.BlockSpec(memory_space=pltpu.VMEM),
        ],
        out_specs=(pl.BlockSpec(memory_space=pl.ANY), pl.BlockSpec(memory_space=pl.ANY)),
        scratch_shapes=[
            pltpu.VMEM((EXPERTS * CAP, width), d_out.dtype),
            pltpu.VMEM((slots, width), d_out.dtype),
            pltpu.VMEM((most, columns), hidden.dtype),
            pltpu.VMEM((most, width), d_out.dtype),
            dma((n_ep,)), dma((n_ep,)), dma,
            dma((n_y, chunks)), dma((n_y, chunks)),
            dma((chunks,)), dma((chunks,)),
            dma((n_y, chunks)), dma((n_y, chunks)),
            dma((n_y, CORES)), dma((n_y, CORES)),
            dma((chunks + 1,)),
        ],
        compiler_params=pltpu.CompilerParams(
            collective_id=1 + number, has_side_effects=True, vmem_limit_bytes=60 * 1024 * 1024),
        name=f"exchange_{number}",
    )(sel, d_out, router, live, hidden)


def on_device(d_out, routes, combine, live_tokens, hidden):
    n_grp, n_ep = lax.axis_size("grp"), lax.axis_size("ep")
    slots = hidden.shape[0]
    step = slots // 24
    sizes = ((17 * step, 21 * step), (24 * step, 24 * step))
    router = jnp.concatenate([routes.astype(jnp.float32), combine], axis=1)
    sel, info = share_counts(router, live_tokens, slots, sizes[:-1], n_grp, n_ep)
    branch = info[0, 0].astype(jnp.int32)
    count = info[0, 1]

    def run(number, *operands):
        *sources, count = operands
        all_hidden, all_rows = exchange(number, sizes[number], *sources, n_grp, n_ep)
        total = lax.dot_general(all_rows, all_hidden, (((0,), (0,)), ((), ())), preferred_element_type=jnp.float32)
        return total * lax.rsqrt(1.0 + count)

    branches = [functools.partial(run, n) for n in range(len(sizes))]
    return lax.switch(branch, branches, sel, d_out, router, live_tokens, hidden, count)


def solution(mesh):
    return jax.shard_map(
        on_device,
        mesh=mesh,
        in_specs=(
            P(("grp", "ep"), None),
            P(("grp", "ep"), None),
            P(("grp", "ep"), None),
            P(("grp", "ep")),
            P("grp", "ep"),
        ),
        out_specs=P("grp", "ep"),
        check_vma=False,
    )
```

profile of v0, /device:TPU:0, one launch (start us, length us, event | category | flops | bytes accessed | tf_op | source)
XLA Modules:
  0.0 154.4 jit_solution(15456043870064888025)
XLA Ops:
  0.7 0.7 convert_element_type.7
  1.3 0.7 pad_maximum_fusion
  2.0 0.7 copy.10.router
  2.8 14.4 %share_counts.1 = (bf16[384,384]{1,0:T(8,128)(2,1)S(1)}, f32[8,128]{1,0:T(8,128)}) custom-call(f32[128,4]{1,0:T(8,128)} %copy.10.router, s32[1]{0:T(128)S(6)} %copy.15.live), custom_call_target="tpu_custom_call" | custom-call | tf_op jit(solution)/shard_map/share_counts/pallas_call | solution.py:110
  17.1 1.4 fusion
  19.2 135.3 %conditional.1 = (f32[512,7168]{1,0:T(8,128)}) conditional(s32[]{:T(128)} %bitcast, (bf16[384,384]{1,0:T(8,128)(2,1)S(1)}, bf16[128,2048]{1,0:T(8,128)(2,1)}, f32[128,4]{0,1:T(4,128)S(1)}, s32[1]{0:T(128)}, bf16[384,7168]{1,0:T(8,128)(2,1)}, /*index=5*/f32[]{:T(128)}) %tuple.11, (bf16[384,384]{1,0:T(8,128)(2,1)S(1)}, bf16[128,2048]{1,0:T(8,128)(2,1)}, ...), branch_computations={%region_0.0_spmd, %region_1.0_spmd} | conditional | flops 11277959168 | bytes 38277152 | solution.py:392
  19.9 0.7 copy.11.router
  20.6 117.0 %exchange_0.1 = (bf16[1216,7168]{1,0:T(8,128)(2,1)}, bf16[1216,512]{1,0:T(8,128)(2,1)}) custom-call(bf16[384,384]{1,0:T(8,128)(2,1)S(1)} %get-tuple-element.32.sel, bf16[128,2048]{1,0:T(8,128)(2,1)} %get-tuple-element.33.d_out, f32[128,4]{1,0:T(8,128)} %copy.11.router, s32[1]{0:T(128)} %get-tuple-element.35.live, bf16[384,7168]{1,0:T(8,128)(2,1)} %get-tuple-element.36.hidden), custom_call_target="tpu_custom_call" | custom-call | tf_op jit(solution)/shard_map/cond/branch_0_fun/exchange_0/pallas_call | solution.py:343
  137.7 16.8 %convolution_multiply_fusion = f32[512,7168]{1,0:T(8,128)} fusion(bf16[1216,512]{1,0:T(8,128)(2,1)} %get-tuple-element.37, bf16[1216,7168]{1,0:T(8,128)(2,1)} %get-tuple-element.38, f32[]{:T(128)S(6)} %rsqrt.4), kind=kOutput, calls=%fused_computation | convolution fusion | flops 8929148928 | bytes 33357828 | tf_op jit(solution)/shard_map/cond/branch_0_fun/dot_general | solution.py:388
where the time goes:
time: 155 us; the launch traced here: 154 us
  Pallas kernels  131 us (85%)
  matrix products  16.8 us (11%)
  local copies, waits for them, and re-layouts  2.86 us (2%)
    pallas_call x1, Pallas kernels, exchange(): pl.pallas_call(functools.partial(exchange_kernel, n_grp, n_ep, keep), out...  117 us
    dot_general x1, matrix products, run(): lax.dot_general(all_rows, all_hidden, (((0,), (0,)), ((), ())), preferred...  16.8 us
    pallas_call x1, Pallas kernels, share_counts(): pl.pallas_call(functools.partial(counts_kernel, n_grp, n_ep, ladder), out...  14.4 us

commit v1 on v0

v1 whole, which is shorter than its diff:
```python
import functools

import jax
import jax.numpy as jnp
from jax import lax
from jax.experimental import pallas as pl
from jax.experimental.pallas import tpu as pltpu
from jax.sharding import PartitionSpec as P

EXPERTS = 8
CAP = 48
CORES = 2
EARLY = 16
LANES = 128
MESH = pl.DeviceIdType.MESH
MIB = 1024 * 1024


def pick_chunks(columns, wide):
    return columns // wide if columns % wide == 0 else columns // 256


def early_kernel(n_grp, n_ep, ladder, routes_in, combine_in, live, d_out, hidden, arrived, early, packed, targets, info,
                 routes, combine, held, mixed, cards, table, tokens_in, buffer, staged,
                 card_send, card_recv, tok_send, tok_recv, tab_send, tab_recv, slot_send, slot_recv,
                 far_send, far_recv, own_sem):
    n_y = n_grp // CORES
    grp, ep = lax.axis_index("grp"), lax.axis_index("ep")
    shards = n_ep // EXPERTS
    y, core = grp // CORES, lax.rem(grp, CORES)
    block = tokens_in.shape[2]
    slots, columns = hidden.shape
    tokens = routes.shape[1]
    first_rows = n_ep * EARLY
    barrier = pltpu.get_barrier_semaphore()

    def in_grp(j):
        return {"grp": lax.rem(grp + j, n_grp), "ep": ep}

    def in_ep(j):
        return {"grp": grp, "ep": lax.rem(ep + j, n_ep)}

    def loop(low, high, body):
        def step(j, _):
            body(j)
            return 0

        lax.fori_loop(low, high, step, 0)

    loop(1, n_grp, lambda j: pl.semaphore_signal(barrier, inc=1, device_id=in_grp(j), device_id_type=MESH))
    loop(1, n_ep, lambda j: pl.semaphore_signal(barrier, inc=1, device_id=in_ep(j), device_id_type=MESH))

    router_copies = [
        pltpu.make_async_copy(routes_in, routes, own_sem.at[2]), pltpu.make_async_copy(combine_in, combine, own_sem.at[3])]
    for copy in router_copies:
        copy.start()
    held_copy = pltpu.make_async_copy(hidden, held, own_sem.at[0])
    held_copy.start()

    def token_block(i):
        return d_out.at[:, pl.ds(pl.multiple_of(i * block, LANES), block)]

    tokens_mine = pltpu.make_async_copy(token_block(grp), tokens_in.at[grp], own_sem.at[1])
    tokens_mine.start()

    for copy in router_copies:
        copy.wait()
    alive = jnp.where(lax.broadcasted_iota(jnp.int32, (1, tokens), 1) < live[0], 1.0, 0.0)
    cards[grp, 0:2, :] = routes[...].astype(jnp.float32)
    cards[grp, 2:4, :] = combine[...] * alive
    cards[grp, 4:8, :] = jnp.broadcast_to(alive, (4, tokens))
    pl.semaphore_wait(barrier, n_grp - 1 + n_ep - 1)

    def card_copy(j, owner):
        return pltpu.make_async_remote_copy(
            src_ref=cards.at[owner], dst_ref=cards.at[owner], send_sem=card_send.at[j], recv_sem=card_recv.at[j],
            device_id=in_grp(j), device_id_type=MESH)

    def token_copy(j):
        return pltpu.make_async_remote_copy(
            src_ref=token_block(lax.rem(grp + j, n_grp)), dst_ref=tokens_in.at[grp],
            send_sem=tok_send.at[j], recv_sem=tok_recv.at[j], device_id=in_grp(j), device_id_type=MESH)

    def token_arrival(j):
        here = tokens_in.at[lax.rem(grp - j + n_grp, n_grp)]
        return pltpu.make_async_remote_copy(
            src_ref=here, dst_ref=here, send_sem=tok_send.at[j], recv_sem=tok_recv.at[j],
            device_id=in_grp(j), device_id_type=MESH)

    loop(1, n_grp, lambda j: card_copy(j, grp).start())
    loop(1, n_grp, lambda j: token_copy(j).start())

    def far_copy(j, s, owner):
        return pltpu.make_async_remote_copy(
            src_ref=hidden.at[pl.ds(pl.multiple_of(s * CAP, 16), EARLY), :],
            dst_ref=early.at[owner, pl.ds(pl.multiple_of(s * EARLY, 16), EARLY), :],
            send_sem=far_send.at[j, s], recv_sem=far_recv.at[j, s],
            device_id={"grp": lax.rem(y + j, n_y) * CORES + core, "ep": ep}, device_id_type=MESH)

    for j in range(1, n_y):
        loop(0, n_ep, lambda s: far_copy(j, s, grp).start())

    loop(1, n_grp, lambda j: card_copy(j, lax.rem(grp - j + n_grp, n_grp)).wait_recv())

    expert_rows = lax.broadcasted_iota(jnp.int32, (LANES, tokens), 0).astype(jnp.float32)

    def count_group(g):
        card = cards[g]
        chosen = jnp.where(expert_rows == card[0:1, :], 1.0, 0.0) + jnp.where(expert_rows == card[1:2, :], 1.0, 0.0)
        lives = jnp.broadcast_to(card[4:5, :], (8, tokens))
        table[ep, g] = lax.dot_general(
            lives.astype(jnp.bfloat16), chosen.astype(jnp.bfloat16), (((1,), (1,)), ((), ())),
            preferred_element_type=jnp.float32)

    loop(0, n_grp, count_group)

    def table_copy(j, owner):
        return pltpu.make_async_remote_copy(
            src_ref=table.at[owner], dst_ref=table.at[owner], send_sem=tab_send.at[j], recv_sem=tab_recv.at[j],
            device_id=in_ep(j), device_id_type=MESH)

    loop(1, n_ep, lambda j: table_copy(j, ep).start())

    square = (tokens, tokens)
    earlier = jnp.where(
        lax.broadcasted_iota(jnp.int32, square, 0) < lax.broadcasted_iota(jnp.int32, square, 1), 1.0, 0.0
    ).astype(jnp.bfloat16)
    slot_rows = lax.broadcasted_iota(jnp.int32, (EXPERTS * CAP, tokens), 0).astype(jnp.float32)

    def fill_group(g):
        card = cards[g]
        picks = [card[k : k + 1, :] for k in range(2)]
        chosen = [jnp.where(expert_rows[0:16, :] == pick, 1.0, 0.0) for pick in picks]
        running = jnp.dot(sum(chosen).astype(jnp.bfloat16), earlier, preferred_element_type=jnp.float32)
        tall = jnp.concatenate([card] * (tokens // 8), axis=0).T
        rows = tokens_in[g].astype(jnp.float32)
        total = None
        for k in range(2):
            position = jnp.sum(chosen[k] * running, axis=0, keepdims=True)
            running = running + chosen[k]
            put = jnp.where(slot_rows == picks[k] * CAP + position, 1.0, 0.0).astype(jnp.bfloat16)
            weighted = (rows * tall[:, 2 + k : 3 + k]).astype(jnp.bfloat16)
            term = jnp.dot(put, weighted, preferred_element_type=jnp.float32)
            total = term if total is None else total + term
        buffer[g] = total.astype(buffer.dtype)

    tokens_mine.wait()
    loop(1, n_grp, lambda j: token_arrival(j).wait_recv())
    loop(0, n_grp, fill_group)

    def expert_slots(expert):
        return buffer.at[:, pl.ds(pl.multiple_of(expert * CAP, CAP), CAP), :]

    def slot_place(source):
        return arrived.at[:, pl.ds(pl.multiple_of(source * CAP, CAP), CAP), :]

    def slot_copy(j):
        target = lax.rem(ep + j, n_ep)
        return pltpu.make_async_remote_copy(
            src_ref=expert_slots(target // shards), dst_ref=slot_place(ep),
            send_sem=slot_send.at[j], recv_sem=slot_recv.at[j],
            device_id={"grp": grp, "ep": target}, device_id_type=MESH)

    def slot_arrival(j):
        here = slot_place(lax.rem(ep - j + n_ep, n_ep))
        return pltpu.make_async_remote_copy(
            src_ref=here, dst_ref=here, send_sem=slot_send.at[j], recv_sem=slot_recv.at[j],
            device_id=in_ep(j), device_id_type=MESH)

    loop(1, n_ep, lambda j: slot_copy(j).start())
    slots_mine = pltpu.make_async_copy(expert_slots(ep // shards), slot_place(ep), own_sem.at[1])
    slots_mine.start()
    loop(1, n_ep, lambda j: table_copy(j, lax.rem(ep - j + n_ep, n_ep)).wait_recv())

    mine = lax.broadcasted_iota(jnp.int32, (8, LANES), 1) == ep // shards
    slot = lax.broadcasted_iota(jnp.int32, (8, slots), 1)
    source = slot // CAP
    place = (slot - source * CAP).astype(jnp.float32)

    def target_group(g):
        def one(s, state):
            filled, first, before = state
            amount = jnp.sum(jnp.where(mine, table[s, g], 0.0), axis=1, keepdims=True)
            here = source == s
            filled = filled + jnp.where(here, amount, 0.0)
            first = first + jnp.where(here, before, 0.0)
            return filled, first, before + jnp.maximum(amount - EARLY, 0.0)

        nothing = jnp.zeros((8, slots), jnp.float32)
        state = (nothing, nothing, jnp.zeros((8, 1), jnp.float32))
        for s in range(n_ep):
            state = one(s, state)
        filled, first, _ = state
        staged[g] = jnp.where((place < filled) & (place >= EARLY), first + place - EARLY, -1.0)

    loop(0, n_grp, target_group)
    target = staged[grp, 0:1, :]
    rows = 64 if mixed.shape[0] % 64 == 0 else mixed.shape[0]

    def write(i):
        start = pl.multiple_of(i * rows, rows)
        index = (lax.broadcasted_iota(jnp.int32, (rows, slots), 0) + start).astype(jnp.float32)
        mixed[pl.ds(start, rows), 0:slots] = jnp.where(index == target, 1.0, 0.0).astype(mixed.dtype)

    loop(0, mixed.shape[0] // rows, write)
    held_copy.wait()
    chunks = pick_chunks(columns, 512)
    wide = columns // chunks

    def packed_copy(i):
        part = pl.ds(pl.multiple_of(i * wide, LANES), wide)
        return pltpu.make_async_copy(mixed.at[:, pl.ds(pl.multiple_of(slots + i * wide, LANES), wide)], packed.at[:, part], own_sem.at[2 + i])

    def pack(i):
        part = pl.ds(pl.multiple_of(i * wide, LANES), wide)
        mixed[:, pl.ds(pl.multiple_of(slots + i * wide, LANES), wide)] = jnp.dot(
            mixed[:, 0:slots], held[:, part], preferred_element_type=jnp.float32).astype(packed.dtype)

        @pl.when(i > 0)
        def _():
            packed_copy(i - 1).start()

    loop(0, chunks, pack)

    need = [jnp.zeros((8, LANES), jnp.float32) for _ in range(CORES)]
    count = jnp.zeros((8, LANES), jnp.float32)
    for g in range(n_grp):
        kept = jnp.zeros((8, LANES), jnp.float32)
        for s in range(n_ep):
            kept = kept + jnp.maximum(table[s, g] - EARLY, 0.0)
            count = count + table[s, g]
        need[g % CORES] = jnp.maximum(need[g % CORES], kept)
    count = jnp.sum(jnp.where(mine, count, 0.0), axis=1, keepdims=True)
    need = [jnp.max(n, axis=1, keepdims=True) for n in need]
    branch = jnp.zeros((8, 1), jnp.float32)
    for keep in ladder:
        branch = branch + jnp.where((need[0] <= keep[0]) & (need[1] <= keep[1]), 0.0, 1.0)
    info[0:8, :] = jnp.broadcast_to(count, (8, LANES))
    info[8:16, :] = jnp.broadcast_to(branch, (8, LANES))
    packed_copy(chunks - 1).start()
    targets[...] = staged[...]

    def early_copy(s):
        return pltpu.make_async_copy(
            held.at[pl.ds(pl.multiple_of(s * CAP, 16), EARLY), :],
            early.at[grp, pl.ds(pl.multiple_of(s * EARLY, 16), EARLY), :], own_sem.at[2 + chunks + s])

    loop(0, n_ep, lambda s: early_copy(s).start())
    loop(0, n_ep, lambda s: early_copy(s).wait())
    loop(0, chunks, lambda i: packed_copy(i).wait())
    slots_mine.wait()

    def leave_grp(j):
        card_copy(j, grp).wait_send()
        token_copy(j).wait_send()

    def leave_ep(j):
        table_copy(j, ep).wait_send()
        slot_copy(j).wait_send()
        slot_arrival(j).wait_recv()

    loop(1, n_grp, leave_grp)
    loop(1, n_ep, leave_ep)
    for j in range(1, n_y):
        peer = lax.rem(y - j + n_y, n_y) * CORES + core

        def leave_far(s):
            far_copy(j, s, grp).wait_send()
            far_copy(j, s, peer).wait_recv()

        loop(0, n_ep, leave_far)


def in_hbm(array):
    return pltpu.with_memory_space_constraint(array, pltpu.HBM)


def gather_early(routes, combine, live, d_out, hidden, ladder, n_grp, n_ep):
    n_y = n_grp // CORES
    slots, columns = hidden.shape
    tokens, width = d_out.shape
    block = width // n_grp
    rest = n_ep * (CAP - EARLY)
    chunks = pick_chunks(columns, 512)
    dma = pltpu.SemaphoreType.DMA
    vmem, smem, hbm = (pl.BlockSpec(memory_space=m) for m in (pltpu.VMEM, pltpu.SMEM, pltpu.HBM))
    return pl.pallas_call(
        functools.partial(early_kernel, n_grp, n_ep, ladder),
        out_shape=(
            jax.ShapeDtypeStruct((n_grp, slots, block), d_out.dtype),
            jax.ShapeDtypeStruct((n_grp, n_ep * EARLY, columns), hidden.dtype),
            jax.ShapeDtypeStruct((rest, columns), hidden.dtype),
            jax.ShapeDtypeStruct((n_grp, 8, slots), jnp.float32),
            jax.ShapeDtypeStruct((16, LANES), jnp.float32),
        ),
        in_specs=[hbm, hbm, smem, hbm, hbm],
        out_specs=(hbm, hbm, hbm, vmem, vmem),
        scratch_shapes=[
            pltpu.VMEM((2, tokens), routes.dtype),
            pltpu.VMEM((2, tokens), combine.dtype),
            pltpu.VMEM((slots, columns), hidden.dtype),
            pltpu.VMEM((rest, slots + columns), hidden.dtype),
            pltpu.VMEM((n_grp, 8, tokens), jnp.float32),
            pltpu.VMEM((n_ep, n_grp, 8, LANES), jnp.float32),
            pltpu.VMEM((n_grp, tokens, block), d_out.dtype),
            pltpu.VMEM((n_grp, EXPERTS * CAP, block), d_out.dtype),
            pltpu.VMEM((n_grp, 8, slots), jnp.float32),
            dma((n_grp,)), dma((n_grp,)), dma((n_grp,)), dma((n_grp,)),
            dma((n_ep,)), dma((n_ep,)), dma((n_ep,)), dma((n_ep,)),
            dma((n_y, n_ep)), dma((n_y, n_ep)),
            dma((2 + chunks + n_ep,)),
        ],
        compiler_params=pltpu.CompilerParams(collective_id=0, has_side_effects=True, vmem_limit_bytes=40 * MIB),
        name="gather_early",
    )(in_hbm(routes), in_hbm(combine), live, in_hbm(d_out), in_hbm(hidden))


def rest_kernel(n_grp, n_ep, keep, arrived, early, packed, targets, info, out, whole, turned, slots_in,
                far_send, far_recv, relay_send, relay_recv, near_send, near_recv, first_send, first_recv, own_sem):
    n_y = n_grp // CORES
    grp, ep = lax.axis_index("grp"), lax.axis_index("ep")
    y, core = grp // CORES, lax.rem(grp, CORES)
    pair = keep[0] + keep[1]
    first_rows = early.shape[1]
    base = n_grp * first_rows
    used = base + n_y * pair
    depth = whole.shape[0]
    columns = packed.shape[1]
    slots = arrived.shape[1]
    block = arrived.shape[2]
    chunks = pick_chunks(columns, 512)
    wide = columns // chunks
    barrier = pltpu.get_barrier_semaphore()

    def loop(low, high, body):
        def step(j, _):
            body(j)
            return 0

        lax.fori_loop(low, high, step, 0)

    def mate(which):
        return {"grp": y * CORES + (1 - which), "ep": ep}

    def at_y(j, which):
        return {"grp": lax.rem(y + j, n_y) * CORES + which, "ep": ep}

    def each_core(body):
        for which in range(CORES):
            pl.when(core == which)(functools.partial(body, which))

    def greet(which):
        for j in range(1, n_y):
            pl.semaphore_signal(barrier, inc=1, device_id=at_y(j, which), device_id_type=MESH)
        pl.semaphore_signal(barrier, inc=1, device_id=mate(which), device_id_type=MESH)

    each_core(greet)

    def part(i):
        return pl.ds(pl.multiple_of(i * wide, LANES), wide)

    def span(row, which):
        start = base + row * pair + (0 if which == 0 else keep[0])
        return pl.ds(pl.multiple_of(start, 16), keep[which])

    def first_span(g):
        return pl.ds(pl.multiple_of(g * first_rows, 16), first_rows)

    def far_copy(which, j, i, row):
        return pltpu.make_async_remote_copy(
            src_ref=packed.at[pl.ds(0, keep[which]), part(i)], dst_ref=whole.at[span(row, which), part(i)],
            send_sem=far_send.at[j, i], recv_sem=far_recv.at[j, i], device_id=at_y(j, which), device_id_type=MESH)

    def relay_copy(which, j, i, cell):
        here = whole.at[span(lax.rem(y - j + n_y, n_y), cell), part(i)]
        return pltpu.make_async_remote_copy(
            src_ref=here, dst_ref=here, send_sem=relay_send.at[j, i], recv_sem=relay_recv.at[j, i],
            device_id=mate(which), device_id_type=MESH)

    def near_copy(which):
        return pltpu.make_async_remote_copy(
            src_ref=packed.at[pl.ds(0, keep[which]), :], dst_ref=whole.at[span(y, which), :],
            send_sem=near_send, recv_sem=near_recv, device_id=mate(which), device_id_type=MESH)

    def near_arrival(which):
        here = whole.at[span(y, 1 - which), :]
        return pltpu.make_async_remote_copy(
            src_ref=here, dst_ref=here, send_sem=near_send, recv_sem=near_recv,
            device_id=mate(which), device_id_type=MESH)

    def first_copy(which, row):
        g = row * CORES + which
        return pltpu.make_async_remote_copy(
            src_ref=early.at[g], dst_ref=whole.at[first_span(g), :],
            send_sem=first_send.at[row], recv_sem=first_recv.at[row], device_id=mate(which), device_id_type=MESH)

    def first_arrival(which, row):
        here = whole.at[first_span(row * CORES + (1 - which)), :]
        return pltpu.make_async_remote_copy(
            src_ref=here, dst_ref=here, send_sem=first_send.at[row], recv_sem=first_recv.at[row],
            device_id=mate(which), device_id_type=MESH)

    def own_copy(which):
        return pltpu.make_async_copy(packed.at[pl.ds(0, keep[which]), :], whole.at[span(y, which), :], own_sem.at[0])

    def own_first(which, row):
        g = row * CORES + which
        return pltpu.make_async_copy(early.at[g], whole.at[first_span(g), :], own_sem.at[1 + row])

    def slots_copy(g):
        return pltpu.make_async_copy(arrived.at[g], slots_in.at[g], own_sem.at[1 + n_y + g])

    pl.semaphore_wait(barrier, n_y)

    def begin(which):
        for j in range(1, n_y):
            loop(0, chunks, lambda i: far_copy(which, j, i, y).start())
        near_copy(which).start()
        loop(0, n_y, lambda row: first_copy(which, row).start())

    each_core(begin)
    loop(0, n_grp, lambda g: slots_copy(g).start())

    def begin_own(which):
        own_copy(which).start()
        loop(0, n_y, lambda row: own_first(which, row).start())

    each_core(begin_own)
    if depth > used:
        whole[used:depth, :] = jnp.zeros((depth - used, columns), whole.dtype)
    loop(0, n_grp, lambda g: slots_copy(g).wait())

    per = LANES // EARLY

    def turn_first(i):
        g = i // (first_rows // LANES)
        s = lax.rem(i, first_rows // LANES) * per
        rows = jnp.concatenate(
            [slots_in[g, pl.ds(pl.multiple_of((s + k) * CAP, 16), EARLY), :] for k in range(per)], axis=0)
        turned[:, pl.ds(pl.multiple_of(i * LANES, LANES), LANES)] = rows.astype(jnp.float32).T.astype(turned.dtype)

    loop(0, base // LANES, turn_first)

    def turn_rest(start, groups):
        rows = jnp.zeros((LANES, block), jnp.float32)
        for g, low in groups:
            index = (lax.broadcasted_iota(jnp.int32, (LANES, slots), 0) + (start - low)).astype(jnp.float32)
            pick = jnp.where(index == targets[g, 0:1, :], 1.0, 0.0).astype(jnp.bfloat16)
            rows = rows + jnp.dot(pick, slots_in[g], preferred_element_type=jnp.float32)
        turned[:, start : start + LANES] = rows.T.astype(turned.dtype)

    lows = [base + (g // CORES) * pair + (g % CORES) * keep[0] for g in range(n_grp)]
    for start in range(base, depth, LANES):
        turn_rest(start, [
            (g, low) for g, low in enumerate(lows) if low < start + LANES and low + keep[g % CORES] > start])

    def settle(which):
        own_copy(which).wait()
        near_arrival(which).wait_recv()

        def row_done(row):
            own_first(which, row).wait()
            first_arrival(which, row).wait_recv()

        loop(0, n_y, row_done)

    each_core(settle)
    scale = lax.rsqrt(1.0 + info[0:1, 0:1])

    def step(i):
        def take(which):
            for j in range(1, n_y):
                far_copy(which, j, i, lax.rem(y - j + n_y, n_y)).wait_recv()
                relay_copy(which, j, i, which).start()
            for j in range(1, n_y):
                relay_copy(which, j, i, 1 - which).wait_recv()

        each_core(take)
        out[:, part(i)] = scale * jnp.dot(turned[...], whole[:, part(i)], preferred_element_type=jnp.float32)

    loop(0, chunks, step)

    def finish(which):
        near_copy(which).wait_send()
        loop(0, n_y, lambda row: first_copy(which, row).wait_send())
        for j in range(1, n_y):
            def leave(i):
                far_copy(which, j, i, y).wait_send()
                relay_copy(which, j, i, which).wait_send()

            loop(0, chunks, leave)

    each_core(finish)


def multiply_rest(number, keep, arrived, early, packed, targets, info, n_grp, n_ep):
    n_y = n_grp // CORES
    _, slots, block = arrived.shape
    columns = packed.shape[1]
    used = n_grp * early.shape[1] + n_y * (keep[0] + keep[1])
    depth = -(-used // LANES) * LANES
    chunks = pick_chunks(columns, 512)
    dma = pltpu.SemaphoreType.DMA
    vmem, hbm = (pl.BlockSpec(memory_space=m) for m in (pltpu.VMEM, pltpu.HBM))
    room = 2 * (depth * (columns + block) + n_grp * slots * block) + 6 * MIB
    return pl.pallas_call(
        functools.partial(rest_kernel, n_grp, n_ep, keep),
        out_shape=pltpu.VMEM((block, columns), jnp.float32),
        in_specs=[hbm, hbm, hbm, vmem, vmem],
        out_specs=vmem,
        scratch_shapes=[
            pltpu.VMEM((depth, columns), packed.dtype),
            pltpu.VMEM((block, depth), arrived.dtype),
            pltpu.VMEM((n_grp, slots, block), arrived.dtype),
            dma((n_y, chunks)), dma((n_y, chunks)), dma((n_y, chunks)), dma((n_y, chunks)),
            dma, dma, dma((n_y,)), dma((n_y,)),
            dma((1 + n_y + n_grp,)),
        ],
        compiler_params=pltpu.CompilerParams(
            collective_id=1 + number, has_side_effects=True, vmem_limit_bytes=room),
        name=f"multiply_rest_{number}",
    )(arrived, early, packed, targets, info)


def store_kernel(total, out, sems):
    parts = sems.shape[0]
    rows = total.shape[0] // parts
    copies = [
        pltpu.make_async_copy(total.at[i * rows : (i + 1) * rows], out.at[i * rows : (i + 1) * rows], sems.at[i])
        for i in range(parts)]
    for copy in copies:
        copy.start()
    for copy in copies:
        copy.wait()


def store(total):
    return pl.pallas_call(
        store_kernel,
        out_shape=pltpu.HBM(total.shape, total.dtype),
        in_specs=[pl.BlockSpec(memory_space=pltpu.VMEM)],
        out_specs=pl.BlockSpec(memory_space=pltpu.HBM),
        scratch_shapes=[pltpu.SemaphoreType.DMA((8,))],
        compiler_params=pltpu.CompilerParams(vmem_limit_bytes=MIB),
        name="store",
    )(total)


def on_device(d_out, routes, combine, live_tokens, hidden):
    n_grp, n_ep = lax.axis_size("grp"), lax.axis_size("ep")
    rest = n_ep * (CAP - EARLY)
    step = rest // 16
    sizes = ((9 * step, 13 * step), (9 * step, 14 * step), (16 * step, 16 * step))
    arrived, early, packed, targets, info = gather_early(
        routes.T, combine.T, live_tokens, d_out, hidden, sizes[:-1], n_grp, n_ep)
    branch = info[8, 0].astype(jnp.int32)

    def run(number, *operands):
        return store(multiply_rest(number, sizes[number], *operands, n_grp, n_ep))

    branches = [functools.partial(run, n) for n in range(len(sizes))]
    return lax.switch(branch, branches, arrived, early, packed, targets, info)


def solution(mesh):
    return jax.shard_map(
        on_device,
        mesh=mesh,
        in_specs=(
            P(("grp", "ep"), None),
            P(("grp", "ep"), None),
            P(("grp", "ep"), None),
            P(("grp", "ep")),
            P("grp", "ep"),
        ),
        out_specs=P("grp", "ep"),
        check_vma=False,
    )
```

time: 155 us -> 120 us (0.77)
  matrix products: 16.8 us -> 0 us
  Pallas kernels: 131 us -> 118 us
  local copies, waits for them, and re-layouts: 2.86 us -> 0.51 us
    dot_general x1 -> x0, matrix products: 16.8 us -> none  [run(): lax.dot_general(all_rows, all_hidden, (((0,), (0,)), ((), ())), preferred...]
    pallas_call x2 -> x3, Pallas kernels: 131 us -> 118 us  [the longest x1 58.9 us: multiply_rest(): pl.pallas_call(functools.partial(rest_kernel, n_grp, n_ep, keep), out_sha...]
where the time goes in v1:
time: 120 us
  Pallas kernels  118 us (98%)
  between operations  1.32 us (1%)
    pallas_call x1, Pallas kernels, multiply_rest(): pl.pallas_call(functools.partial(rest_kernel, n_grp, n_ep, keep), out_sha...  58.9 us
    pallas_call x1, Pallas kernels, gather_early(): pl.pallas_call(functools.partial(early_kernel, n_grp, n_ep, ladder), out_...  54.2 us
    pallas_call x1, Pallas kernels, store(): pl.pallas_call(store_kernel, out_shape=pltpu.HBM(total.shape, total.dtype...  5.32 us

profile of v1, /device:TPU:0, one launch (start us, length us, event | category | flops | bytes accessed | tf_op | source)
XLA Modules:
  0.0 120.2 jit_solution(10588831471144404428)
XLA Ops:
  0.7 54.2 %gather_early.1 = (bf16[4,384,512]{2,1,0:T(8,128)(2,1)S(1)}, bf16[4,128,7168]{2,1,0:T(8,128)(2,1)S(1)}, bf16[256,7168]{1,0:T(8,128)(2,1)S(1)}, f32[4,8,384]{2,1,0:T(8,128)S(1)}, f32[16,128]{1,0:T(8,128)S(1)}) custom-call(s32[2,128]{1,0:T(2,128)} %bitcast.3, f32[2,128]{1,0:T(2,128)} %bitcast.4, s32[1]{0:T(128)S(6)} %copy.12.live, bf16[128,2048]{1,0:T(8,128)(2,1)} %d_out.1, ...), custom_call_target="tpu_custom_call" | custom-call | tf_op jit(solution)/shard_map/gather_early/pallas_call | solution.py:287
  54.8 0.5 slice.3
  56.0 64.2 %conditional.1 = (f32[512,7168]{1,0:T(8,128)}) conditional(s32[]{:T(128)} %bitcast.2, (bf16[4,384,512]{2,1,0:T(8,128)(2,1)S(1)}, bf16[4,128,7168]{2,1,0:T(8,128)(2,1)S(1)}, bf16[256,7168]{1,0:T(8,128)(2,1)S(1)}, f32[4,8,384]{2,1,0:T(8,128)S(1)}, f32[16,128]{1,0:T(8,128)S(1)}) %gather_early.1, (bf16[4,384,512]{2,1,0:T(8,128)(2,1)S(1)}, ...), branch_computations={%region_0.0_spmd, %region_1.0_spmd, %region_2.0_spmd} | conditional | bytes 8 | solution.py:562
  56.0 58.9 %multiply_rest_0.1.total = f32[512,7168]{1,0:T(8,128)S(1)} custom-call(bf16[4,384,512]{2,1,0:T(8,128)(2,1)S(1)} %get-tuple-element.38.arrived, bf16[4,128,7168]{2,1,0:T(8,128)(2,1)S(1)} %get-tuple-element.40.early, bf16[256,7168]{1,0:T(8,128)(2,1)S(1)} %get-tuple-element.41.packed, f32[4,8,384]{2,1,0:T(8,128)S(1)} %get-tuple-element.42.targets, ...), custom_call_target="tpu_custom_call" | custom-call | tf_op jit(solution)/shard_map/cond/branch_0_fun/multiply_rest_0/pallas_call | solution.py:506
  114.9 5.3 %store.3 = f32[512,7168]{1,0:T(8,128)} custom-call(f32[512,7168]{1,0:T(8,128)S(1)} %multiply_rest_0.1.total), custom_call_target="tpu_custom_call" | custom-call | tf_op jit(solution)/shard_map/cond/branch_0_fun/store/pallas_call | solution.py:538
